TPU v7x, 256 devices: a whole 4x4x8 slice. The times are simulated.
256 devices in a mesh: bl: 32 (over z, x), tm: 8 (over y, core).
Axes of the slice: x: 4, y: 4, z: 8, core: 2. Of those that a mesh axis runs over, the one named last changes fastest.
Arguments:
- visibility_real: bfloat16 [12288, 32, 1024], P('bl', 'tm'), may hold values from -6 to 6
- visibility_imag: bfloat16 [12288, 32, 1024], P('bl', 'tm'), may hold values from -6 to 6
- weights: int32 [12288, 32], P('bl', 'tm'), may hold values from 0 to 8
- labels: int32 [12288], P('bl'), may hold values from 0 to 2047, as said below
- owner_of: int32 [2048], replicated, may hold values from 0 to 31, as said below
Outputs:
- bandpower: float32 [2048, 1024], P(('bl', 'tm'))
Inputs may be any that keep to these rules, and one draw needn't show every extreme that they name: Of the rows of one device, at most 18 have labels of groups with one owner, and these carry at most 4 different labels; in every draw some owner gets exactly 18 such rows with exactly 4 labels from every device. `owner_of`: every owner owns exactly 64 groups.
All inputs are finite; a program needn't handle non-finite values.
Results may differ from a plain program's by a relative error of at most 0.0003.
Values may be sent and summed in bfloat16 or wider, within the bound.
A program may use at most 128 MiB of HBM per device.

v0:
```python
import math

import jax
import jax.numpy as jnp
from jax import lax
from jax.sharding import PartitionSpec as P

HARRIS = (0.35875, 0.48829, 0.14128, 0.01168)


def from_behind(block, axis, distance):
    devices = range(lax.axis_size(axis))
    route = [(i - distance, i) for i in devices if i - distance in devices]
    return lax.ppermute(block, axis, route)


def in_blocks(x, dim, size):
    before, after = (x.shape[:dim], x.shape[dim + 1 :])
    return jnp.moveaxis(x.reshape(*before, size, -1, *after), dim, 0)


def summed_on_arrival(x, axis, dim):
    size = lax.axis_size(axis)
    blocks = lax.all_to_all(in_blocks(x, dim, size), axis, 0, 0, tiled=True)
    return jnp.sum(blocks, axis=0)


def taper_of(length):
    phase_angle = 2.0 * math.pi / length * jnp.arange(length, dtype=jnp.float32)
    return (
        HARRIS[0]
        - HARRIS[1] * jnp.cos(phase_angle)
        + HARRIS[2] * jnp.cos(2.0 * phase_angle)
        - HARRIS[3] * jnp.cos(3.0 * phase_angle)
    )


def dft_tables(channels):
    window_taper = taper_of(channels)
    window_taper = window_taper / jnp.sqrt(jnp.sum(window_taper * window_taper))
    channel_index = jnp.arange(channels, dtype=jnp.int32)
    phase_turns = channel_index[:, None] * channel_index[None, :] % channels
    phase_angle = 2.0 * math.pi / channels * phase_turns.astype(jnp.float32)
    cosine = jnp.cos(phase_angle) * window_taper[:, None]
    sine_part = jnp.sin(phase_angle) * window_taper[:, None]
    table_real = jnp.concatenate([cosine, -sine_part], axis=1)
    table_imag = jnp.concatenate([sine_part, cosine], axis=1)
    return (table_real, table_imag)


def owner_rank(owner_of, owners):
    owner_hits = (owner_of[:, None] == jnp.arange(owners, dtype=jnp.int32)[None, :]).astype(
        jnp.int32
    )
    earlier = jnp.cumsum(owner_hits, axis=0) - owner_hits
    return jnp.sum(earlier * owner_hits, axis=1)


def per_device(visibility_real, visibility_imag, weights, labels, owner_of):
    row_count, resident_times, channels = visibility_real.shape
    owners = lax.axis_size("bl")
    groups = owner_of.shape[0]
    per_owner = groups // owners
    capacity = 3 * row_count // (2 * owners)
    distinct = min(capacity // 4, per_owner // 2)
    table_real, table_imag = dft_tables(channels)
    group_rank = owner_rank(owner_of, owners)
    label_match = labels[:, None] == jnp.arange(groups, dtype=jnp.int32)[None, :]
    row_owner = jnp.sum(jnp.where(label_match, owner_of[None, :], 0), axis=1)
    row_rank = jnp.sum(jnp.where(label_match, group_rank[None, :], 0), axis=1)
    group_index = jnp.arange(per_owner, dtype=jnp.int32)[:, None, None]
    local_key = row_owner * per_owner + row_rank
    key_match = local_key[:, None] == jnp.arange(groups, dtype=jnp.int32)[None, :]
    present = jnp.any(key_match, axis=0).astype(jnp.int32).reshape(owners, per_owner)
    order_within = jnp.cumsum(present, axis=1) - present
    slot_of_key = (jnp.arange(owners, dtype=jnp.int32)[:, None] * distinct + order_within).reshape(
        groups
    )
    row_slot = jnp.sum(jnp.where(key_match, slot_of_key[None, :], 0), axis=1)
    slot_hit = (
        order_within[:, :, None] == jnp.arange(distinct, dtype=jnp.int32)[None, None, :]
    ) & (present[:, :, None] > 0)
    slot_rank = jnp.sum(
        jnp.where(slot_hit, jnp.arange(per_owner, dtype=jnp.int32)[None, :, None], 0), axis=1
    )
    send_rank = jnp.broadcast_to(slot_rank[:, :, None], (owners, distinct, resident_times))
    slot_weight = jnp.where(
        row_slot[None, :, None] == jnp.arange(owners * distinct, dtype=jnp.int32)[:, None, None],
        weights[None],
        0,
    )
    folder = slot_weight.astype(jnp.bfloat16)
    part_real = jnp.einsum(
        "krt,rtf->ktf", folder, visibility_real, preferred_element_type=jnp.float32
    ).reshape(owners, distinct, resident_times, channels)
    part_imag = jnp.einsum(
        "krt,rtf->ktf", folder, visibility_imag, preferred_element_type=jnp.float32
    ).reshape(owners, distinct, resident_times, channels)
    part_weight = (
        jnp.sum(slot_weight, axis=1).astype(jnp.float32).reshape(owners, distinct, resident_times)
    )
    received_real = lax.all_to_all(part_real, "bl", split_axis=0, concat_axis=0, tiled=True)
    came_imag = lax.all_to_all(part_imag, "bl", split_axis=0, concat_axis=0, tiled=True)
    came_weight = lax.all_to_all(part_weight, "bl", split_axis=0, concat_axis=0, tiled=True)
    came_rank = lax.all_to_all(send_rank, "bl", split_axis=0, concat_axis=0, tiled=True)
    items = received_real.shape[2]
    flat_real = received_real.reshape(-1, items, channels)
    flat_imag = came_imag.reshape(-1, items, channels)
    flat_weight = came_weight.reshape(-1, items)
    flat_rank = came_rank.reshape(-1, items)
    selector = (flat_rank[None] == group_index).astype(jnp.float32)
    sum_real = jnp.einsum("gsn,snf->gnf", selector, flat_real, precision=lax.Precision.HIGHEST)
    sum_imag = jnp.einsum("gsn,snf->gnf", selector, flat_imag, precision=lax.Precision.HIGHEST)
    weight_sum = jnp.sum(selector * flat_weight[None], axis=1)
    divisor = jnp.maximum(weight_sum, 1.0)[:, :, None]
    mean_real = sum_real / divisor
    mean_imag = sum_imag / divisor
    arrived_result = jnp.einsum(
        "gnf,fk->gnk", mean_real, table_real, precision=lax.Precision.HIGHEST
    ) + jnp.einsum("gnf,fk->gnk", mean_imag, table_imag, precision=lax.Precision.HIGHEST)
    following = from_behind(arrived_result[:, 0, :], "tm", -1)
    pair_sum = (
        jnp.sum(arrived_result[:, :-1, :] * arrived_result[:, 1:, :], axis=1)
        + arrived_result[:, -1, :] * following
    )
    partial_power = pair_sum[:, :channels] + pair_sum[:, channels:]
    return summed_on_arrival(partial_power, "tm", 0)


def solution(mesh):
    placed = (P("bl", "tm", None), P("bl", "tm", None), P("bl", "tm"), P("bl"), P())
    return jax.shard_map(
        per_device, mesh=mesh, in_specs=placed, out_specs=P(("bl", "tm"), None), check_vma=False
    )
```

profile of v0, /device:TPU:1, one launch (start us, length us, event | category | flops | bytes accessed | tf_op | source)
XLA Modules:
  0.0 220.2 jit_solution(9648480874031671634)
XLA Ops:
  0.0 1.6 fusion.40
  1.6 15.9 %reduce-window.6 = s32[32,16,128]{2,1,0:T(8,128)S(1)} reduce-window(s32[32,16,128]{2,1,0:T(8,128)} %fusion.40, s32[]{:T(128)} %constant.16.clone.1), window={size=1x1x128 pad=0_0x0_0x127_0}, to_apply=%region_1.2 | reduce-window | flops 8323072 | bytes 524292 | tf_op jit(solution)/shard_map/reduce-window
  17.5 0.8 slice.32
  18.3 1.2 copy.51
  19.5 0.2 reduce-window.9
  19.7 0.1 broadcast_add_fusion
  19.8 0.8 fusion.38
  20.6 1.7 select_reduce_fusion.2
  22.4 0.6 fusion.16
  23.1 0.2 reduce_window_sum.30
  23.3 0.1 select_reduce_fusion.5
  23.5 0.6 broadcast_in_dim.92
  24.2 11.9 %all-to-all-start.1 = ((s32[32,4,4]{1,2,0:T(4,128)}), s32[32,4,4]{1,2,0:T(4,128)S(1)}, u32[]{:S(2)}, u32[]{:S(2)}) async-start(s32[32,4,4]{1,2,0:T(4,128)} %broadcast_in_dim.92), calls=%async_computation.1 | async-start | bytes 131072 | tf_op jit(solution)/shard_map/all_to_all | solution.py:105
  36.3 0.6 select_reduce_fusion
  36.9 0.8 select_reduce_fusion.3
  37.7 0.1 convert_element_type.51
  37.8 0.7 copy.46
  38.5 6.3 %all-to-all-done.1 = s32[32,4,4]{1,2,0:T(4,128)S(1)} async-done(((s32[32,4,4]{1,2,0:T(4,128)}), s32[32,4,4]{1,2,0:T(4,128)S(1)}, u32[]{:S(2)}, u32[]{:S(2)}) %all-to-all-start.1) | async-done | bytes 2080 | tf_op jit(solution)/shard_map/all_to_all | solution.py:105
  44.9 3.8 %all-to-all-start.2 = ((f32[32,4,4]{1,2,0:T(4,128)}), f32[32,4,4]{1,2,0:T(4,128)S(1)}, u32[]{:S(2)}, u32[]{:S(2)}) async-start(f32[32,4,4]{1,2,0:T(4,128)} %copy.46), calls=%async_computation.2 | async-start | bytes 131072 | tf_op jit(solution)/shard_map/all_to_all | solution.py:104
  48.7 3.5 %fusion.18 = f32[128,4,1024]{2,0,1:T(8,128)} fusion(bf16[384,4,1024]{2,1,0:T(4,128)(2,1)S(1)} %copy-done, s32[384,4]{0,1:T(4,128)S(1)} %copy-done.3, pred[128,384]{1,0:T(8,128)(4,1)S(1)} %iota_compare_fusion.4), kind=kOutput, calls=%fused_computation.30 | convolution fusion | flops 403046400 | bytes 5298176 | tf_op jit(solution)/shard_map/krt,rtf->ktf/dot_general | solution.py:93
  52.2 2.8 %reshape.130 = f32[32,4,4,1024]{3,1,0,2:T(4,128)} reshape(f32[128,4,1024]{2,0,1:T(8,128)} %fusion.18) | data formatting | bytes 4194304 | tf_op jit(solution)/shard_map/reshape | solution.py:95
  55.0 3.2 %copy.42 = f32[32,4,4,1024]{3,1,2,0:T(4,128)} copy(f32[32,4,4,1024]{3,1,0,2:T(4,128)} %reshape.130) | data formatting | bytes 4194304 | tf_op jit(solution)/shard_map/reshape | solution.py:95
  58.2 9.3 %all-to-all-start = ((f32[32,4,4,1024]{3,1,2,0:T(4,128)}), f32[32,4,4,1024]{3,1,2,0:T(4,128)}, u32[]{:S(2)}, u32[]{:S(2)}) async-start(f32[32,4,4,1024]{3,1,2,0:T(4,128)} %copy.42), calls=%async_computation | async-start | bytes 4194304 | tf_op jit(solution)/shard_map/all_to_all | solution.py:102
  67.6 5.3 %fusion.21 = f32[128,4,1024]{2,0,1:T(8,128)} fusion(bf16[384,4,1024]{2,1,0:T(4,128)(2,1)} %param.6, s32[384,4]{0,1:T(4,128)S(1)} %copy-done.3, pred[128,384]{1,0:T(8,128)(4,1)S(1)} %iota_compare_fusion.4), kind=kOutput, calls=%fused_computation.31 | convolution fusion | flops 403046400 | bytes 5298176 | tf_op jit(solution)/shard_map/krt,rtf->ktf/dot_general | solution.py:96
  72.9 2.8 %reshape.132 = f32[32,4,4,1024]{3,1,0,2:T(4,128)} reshape(f32[128,4,1024]{2,0,1:T(8,128)} %fusion.21) | data formatting | bytes 4194304 | tf_op jit(solution)/shard_map/reshape | solution.py:98
  75.8 3.2 %copy.49 = f32[32,4,4,1024]{3,1,2,0:T(4,128)} copy(f32[32,4,4,1024]{3,1,0,2:T(4,128)} %reshape.132) | data formatting | bytes 4194304 | tf_op jit(solution)/shard_map/reshape | solution.py:98
  78.9 34.7 %all-to-all-done = f32[32,4,4,1024]{3,1,2,0:T(4,128)} async-done(((f32[32,4,4,1024]{3,1,2,0:T(4,128)}), f32[32,4,4,1024]{3,1,2,0:T(4,128)}, u32[]{:S(2)}, u32[]{:S(2)}) %all-to-all-start) | async-done | bytes 2097184 | tf_op jit(solution)/shard_map/all_to_all | solution.py:102
  113.6 7.8 %all-to-all-start.3 = ((f32[32,4,4,1024]{3,1,2,0:T(4,128)}), f32[32,4,4,1024]{3,1,2,0:T(4,128)}, u32[]{:S(2)}, u32[]{:S(2)}) async-start(f32[32,4,4,1024]{3,1,2,0:T(4,128)} %copy.49), calls=%async_computation.3 | async-start | bytes 4194304 | tf_op jit(solution)/shard_map/all_to_all | solution.py:103
  121.4 0.7 multiply_reduce_fusion
  122.8 19.6 %sine_multiply_fusion = (f32[1024,1024]{1,0:T(8,128)}, f32[1024,1024]{1,0:T(8,128)}, f32[1024,1024]{1,0:T(8,128)}) fusion(f32[1024]{0:T(1024)S(1)} %fusion.53), kind=kLoop, calls=%fused_computation.14 | loop fusion | flops 17825792 | bytes 12587008 | tf_op jit(solution)/shard_map/mul | solution.py:45
  142.4 0.1 eq.116
  142.5 0.1 mul.161
  142.6 0.1 select_reduce_fusion.4
  142.7 3.1 %copy.43 = f32[32,4,4,1024]{3,1,0,2:T(4,128)} copy(f32[32,4,4,1024]{3,1,2,0:T(4,128)} %all-to-all-done) | data formatting | bytes 4194304 | tf_op jit(solution)/shard_map/all_to_all | solution.py:102
  145.9 2.9 %reshape.131 = f32[128,4,1024]{2,0,1:T(8,128)} reshape(f32[32,4,4,1024]{3,1,0,2:T(4,128)} %copy.43) | data formatting | bytes 4194304 | tf_op jit(solution)/shard_map/reshape | solution.py:107
  148.8 17.3 %all-to-all-done.3 = f32[32,4,4,1024]{3,1,2,0:T(4,128)} async-done(((f32[32,4,4,1024]{3,1,2,0:T(4,128)}), f32[32,4,4,1024]{3,1,2,0:T(4,128)}, u32[]{:S(2)}, u32[]{:S(2)}) %all-to-all-start.3) | async-done | bytes 2097184 | tf_op jit(solution)/shard_map/all_to_all | solution.py:103
  166.1 3.1 %copy.50 = f32[32,4,4,1024]{3,1,0,2:T(4,128)} copy(f32[32,4,4,1024]{3,1,2,0:T(4,128)} %all-to-all-done.3) | data formatting | bytes 4194304 | tf_op jit(solution)/shard_map/all_to_all | solution.py:103
  169.2 3.0 %reshape.133 = f32[128,4,1024]{2,0,1:T(8,128)} reshape(f32[32,4,4,1024]{3,1,0,2:T(4,128)} %copy.50) | data formatting | bytes 4194304 | tf_op jit(solution)/shard_map/reshape | solution.py:108
  172.2 2.6 %fusion.27 = f32[64,4,1024]{2,0,1:T(8,128)S(1)} fusion(f32[128,4,1024]{2,0,1:T(8,128)} %reshape.131, f32[64,4]{0,1:T(4,128)S(1)} %broadcast_maximum_fusion, s32[128,4]{0,1:T(4,128)S(1)} %eq.116), kind=kOutput, calls=%fused_computation.38 | convolution fusion | flops 402948096 | bytes 3148800 | tf_op jit(solution)/shard_map/gsn,snf->gnf/dot_general | solution.py:112
  174.8 2.4 %fusion.26 = f32[64,4,1024]{2,0,1:T(8,128)S(1)} fusion(f32[128,4,1024]{2,0,1:T(8,128)} %reshape.133, f32[64,4]{0,1:T(4,128)S(1)} %broadcast_maximum_fusion, s32[128,4]{0,1:T(4,128)S(1)} %eq.116), kind=kOutput, calls=%fused_computation.36 | convolution fusion | flops 402948096 | bytes 3148800 | tf_op jit(solution)/shard_map/gsn,snf->gnf/dot_general | solution.py:113
  177.3 8.2 %fusion = f32[64,4,2048]{2,0,1:T(8,128)S(1)} fusion(f32[64,4,1024]{2,0,1:T(8,128)S(1)} %fusion.27, f32[1024,1024]{1,0:T(8,128)} %get-tuple-element.8, f32[1024,1024]{1,0:T(8,128)S(1)} %copy-done.1), kind=kOutput, calls=%fused_computation.1 | convolution fusion | flops 6444548096 | bytes 11534336 | tf_op jit(solution)/shard_map/gnf,fk->gnk/dot_general | solution.py:118
  185.5 7.4 %fusion.17 = f32[64,4,2048]{2,0,1:T(8,128)S(1)} fusion(f32[64,4,2048]{2,0,1:T(8,128)S(1)} %fusion, f32[64,4,1024]{2,0,1:T(8,128)S(1)} %fusion.26, f32[1024,1024]{1,0:T(8,128)S(1)} %copy-done.1, f32[1024,1024]{1,0:T(8,128)S(1)} %copy-done.2), kind=kOutput, calls=%fused_computation.29 | convolution fusion | flops 6445072384 | bytes 13631488 | tf_op jit(solution)/shard_map/gnf,fk->gnk/dot_general | solution.py:120
  193.0 7.8 %collective-permute-start = (f32[64,2048]{1,0:T(8,128)S(1)}, f32[64,2048]{1,0:T(8,128)S(1)}, u32[]{:S(2)}, u32[]{:S(2)}) collective-permute-start(f32[64,2048]{1,0:T(8,128)S(1)} %slice_bitcast_fusion), channel_id=1, source_target_pairs={{1,0},{2,1},{3,2},{4,3},{5,4},{6,5},{7,6},{9,8},{10,9},{11,10},{12... | collective-permute-start | bytes 1572872 | tf_op jit(solution)/shard_map/ppermute | solution.py:14
  200.8 0.2 fusion.25
  201.1 7.8 %collective-permute-done = f32[64,2048]{1,0:T(8,128)S(1)} collective-permute-done((f32[64,2048]{1,0:T(8,128)S(1)}, f32[64,2048]{1,0:T(8,128)S(1)}, u32[]{:S(2)}, u32[]{:S(2)}) %collective-permute-start) | collective-permute-done | bytes 524320 | tf_op jit(solution)/shard_map/ppermute | solution.py:14
  208.9 0.1 fusion.29
  209.0 10.5 %all_to_all.25 = f32[8,8,1024]{2,1,0:T(8,128)S(1)} all-to-all(f32[8,8,1024]{2,1,0:T(8,128)S(1)} %fusion.39), channel_id=1, replica_groups=mesh['bl'=32,'tm'=8] {'tm'}, dimensions={0} | all-to-all | bytes 524288 | tf_op jit(solution)/shard_map/all_to_all | solution.py:24
  219.6 0.6 reduce_sum.99
  (28 shorter events, 0.6 us)
Async XLA Ops:
  0.0 48.7 %copy-start = (bf16[384,4,1024]{2,1,0:T(4,128)(2,1)S(1)}, bf16[384,4,1024]{2,1,0:T(4,128)(2,1)}, u32[]{:S(2)}) copy-start(bf16[384,4,1024]{2,1,0:T(4,128)(2,1)} %param.5) | copy-start | bytes 9437188
  0.0 48.7 %copy-start.3 = (s32[384,4]{0,1:T(4,128)S(1)}, s32[384,4]{0,1:T(4,128)}, u32[]{:S(2)}) copy-start(s32[384,4]{0,1:T(4,128)} %param.7) | copy-start | bytes 18436
  24.2 20.7 %all-to-all-start.1 = ((s32[32,4,4]{1,2,0:T(4,128)}), s32[32,4,4]{1,2,0:T(4,128)S(1)}, u32[]{:S(2)}, u32[]{:S(2)}) async-start(s32[32,4,4]{1,2,0:T(4,128)} %broadcast_in_dim.92), calls=%async_computation.1 | async-start | bytes 131072 | tf_op jit(solution)/shard_map/all_to_all | solution.py:105
  44.9 13.4 %all-to-all-start.2 = ((f32[32,4,4]{1,2,0:T(4,128)}), f32[32,4,4]{1,2,0:T(4,128)S(1)}, u32[]{:S(2)}, u32[]{:S(2)}) async-start(f32[32,4,4]{1,2,0:T(4,128)} %copy.46), calls=%async_computation.2 | async-start | bytes 131072 | tf_op jit(solution)/shard_map/all_to_all | solution.py:104
  58.2 55.4 %all-to-all-start = ((f32[32,4,4,1024]{3,1,2,0:T(4,128)}), f32[32,4,4,1024]{3,1,2,0:T(4,128)}, u32[]{:S(2)}, u32[]{:S(2)}) async-start(f32[32,4,4,1024]{3,1,2,0:T(4,128)} %copy.42), calls=%async_computation | async-start | bytes 4194304 | tf_op jit(solution)/shard_map/all_to_all | solution.py:102
  113.6 52.5 %all-to-all-start.3 = ((f32[32,4,4,1024]{3,1,2,0:T(4,128)}), f32[32,4,4,1024]{3,1,2,0:T(4,128)}, u32[]{:S(2)}, u32[]{:S(2)}) async-start(f32[32,4,4,1024]{3,1,2,0:T(4,128)} %copy.49), calls=%async_computation.3 | async-start | bytes 4194304 | tf_op jit(solution)/shard_map/all_to_all | solution.py:103
  172.2 5.1 %copy-start.1 = (f32[1024,1024]{1,0:T(8,128)S(1)}, f32[1024,1024]{1,0:T(8,128)}, u32[]{:S(2)}) copy-start(f32[1024,1024]{1,0:T(8,128)} %get-tuple-element.9) | copy-start | bytes 12582916
  177.3 8.3 %copy-start.2 = (f32[1024,1024]{1,0:T(8,128)S(1)}, f32[1024,1024]{1,0:T(8,128)}, u32[]{:S(2)}) copy-start(f32[1024,1024]{1,0:T(8,128)} %get-tuple-element.7) | copy-start | bytes 12582916
  193.0 15.9 %collective-permute-start = (f32[64,2048]{1,0:T(8,128)S(1)}, f32[64,2048]{1,0:T(8,128)S(1)}, u32[]{:S(2)}, u32[]{:S(2)}) collective-permute-start(f32[64,2048]{1,0:T(8,128)S(1)} %slice_bitcast_fusion), channel_id=1, source_target_pairs={{1,0},{2,1},{3,2},{4,3},{5,4},{6,5},{7,6},{9,8},{10,9},{11,10},{12... | collective-permute-start | bytes 1572872 | tf_op jit(solution)/shard_map/ppermute | solution.py:14
where the time goes:
time: 222 us; the launch traced here: 220 us
  waiting for transfers between devices  66.1 us (30%)
  other arithmetic  44.2 us (20%)
  starting transfers between devices  40.7 us (18%)
  matrix products  29.5 us (13%)
  local copies, waits for them, and re-layouts  28.3 us (13%)
  blocking collectives  10.5 us (5%)
    all_to_all x1, waiting for transfers between devices, per_device(): lax.all_to_all(part_real, 'bl', split_axis=0, concat_axis=0, tiled=True)  34.7 us
    mul x1, other arithmetic, dft_tables(): sine_part = jnp.sin(phase_angle) * window_taper[:, None]  19.6 us
    all_to_all x1, waiting for transfers between devices, per_device(): lax.all_to_all(part_imag, 'bl', split_axis=0, concat_axis=0, tiled=True)  17.3 us
    another operation x3, other arithmetic  16.2 us
    all_to_all x1, starting transfers between devices, per_device(): lax.all_to_all(send_rank, 'bl', split_axis=0, concat_axis=0, tiled=True)  11.9 us
    all_to_all x1, blocking collectives, summed_on_arrival(): blocks = lax.all_to_all(in_blocks(x, dim, size), axis, 0, 0, tiled=True)  10.5 us
    all_to_all x1, starting transfers between devices, per_device(): lax.all_to_all(part_real, 'bl', split_axis=0, concat_axis=0, tiled=True)  9.34 us
    dot_general x1, matrix products, per_device(): jnp.einsum('gnf,fk->gnk', mean_real, table_real, precision=lax.Precision....  8.23 us
  transfers between devices with their start and end apart: 5, of which 4 were waited for; matrix products, arithmetic and copies ran while one was open for 23% of the time, Pallas kernels for 0%

commit v1 on v0

v1 whole, which is shorter than its diff:
```python
import functools
import math

import jax
import jax.numpy as jnp
import numpy as np
from jax import lax
from jax.experimental import pallas as pl
from jax.experimental.pallas import tpu as pltpu
from jax.sharding import PartitionSpec as P

HARRIS = (0.35875, 0.48829, 0.14128, 0.01168)
MESH = pl.DeviceIdType.MESH
F32, BF16, I32 = jnp.float32, jnp.bfloat16, jnp.int32

OFFSETS = [
    (dz, dx) for dx in (0, 1, 2, 3) for dz in (1, 7, 2, 6, 3, 5, 4, 0) if (dz, dx) != (0, 0)
]


def taper_row(length):
    angle = 2.0 * np.pi / length * np.arange(length)
    h = (
        HARRIS[0]
        - HARRIS[1] * np.cos(angle)
        + HARRIS[2] * np.cos(2.0 * angle)
        - HARRIS[3] * np.cos(3.0 * angle)
    )
    return (h / np.sqrt(np.sum(h * h)))[None, :].astype(np.float32)


def dft_constants(length):
    n = length // 4
    angle = 2.0 * np.pi / n * (np.outer(np.arange(n), np.arange(n)) % n)
    c, s = np.cos(angle), np.sin(angle)
    table = np.block([[c, -s], [s, c]]).astype(np.float32)
    high = table.astype(jnp.bfloat16)
    low = (table - high.astype(np.float32)).astype(jnp.bfloat16)
    turn = 2.0 * np.pi / length * np.outer(np.arange(4), np.arange(n))
    twiddle = np.concatenate([np.cos(turn), np.sin(turn)], axis=0).astype(np.float32)
    return high, low, twiddle


def iota(shape, dim):
    return lax.broadcasted_iota(I32, shape, dim)


def dot(a, b):
    return jnp.dot(a, b, preferred_element_type=F32)


def dot_t(a, b):
    return lax.dot_general(a, b, (((1,), (1,)), ((), ())), preferred_element_type=F32)


def index_rows(labels_ref, owner_ref, sel):
    rows = labels_ref.shape[1]
    blocks = owner_ref.shape[1] // 128
    columns = []
    for b in range(rows // 128):
        piece = labels_ref[:, 128 * b : 128 * b + 128].astype(F32)
        columns.append(jnp.transpose(jnp.broadcast_to(piece, (128, 128))))
    label_col = jnp.concatenate(columns, axis=0)
    lane = iota((rows, 128), 1).astype(F32)
    owner_iota = iota((32, 128), 0)
    hits, marks = [], []
    for b in range(blocks):
        chosen = (label_col == lane + 128.0 * b).astype(F32)
        sel[:, 128 * b : 128 * b + 128] = chosen.astype(BF16)
        present = jnp.max(chosen, axis=0, keepdims=True)
        hit = (owner_ref[:, 128 * b : 128 * b + 128] == owner_iota).astype(F32)
        hits.append(hit)
        marks.append(hit)
        marks.append(hit * present)
    stacked = jnp.concatenate(marks, axis=0).astype(BF16)
    earlier = jnp.logical_or(iota((128, 256), 0) < iota((128, 256), 1), iota((128, 256), 1) >= 128)
    sums = dot(stacked, earlier.astype(F32).astype(BF16))
    before = jnp.zeros((64, 128), F32)
    row8 = iota((8, 128), 0)
    tables = []
    for b in range(blocks):
        within = sums[64 * b : 64 * b + 64]
        prefix = within[:, :128] + before
        before = before + within[:, 128:]
        rank = jnp.sum(hits[b] * prefix[:32], axis=0, keepdims=True)
        slot = jnp.sum(hits[b] * (prefix[32:] + 4.0 * owner_iota.astype(F32)), axis=0, keepdims=True)
        tables.append(jnp.where(row8 == 0, slot, jnp.where(row8 == 1, rank, 0.0)))
    table = jnp.concatenate(tables, axis=1).astype(BF16)
    return dot_t(table, sel[...])


def kernel(
    labels_ref, owner_ref, weights_ref, taper_ref, twiddle_ref, vis_re, vis_im, high_hbm, low_hbm,
    out_ref,
    raw, flat, sel, sent, held, meta_out, meta_in, table, first, after, parts, fb,
    load_sem, send_sem, recv_sem, meta_send, meta_recv, edge_send, edge_recv, part_send, part_recv,
):
    bl, tm = lax.axis_index("bl"), lax.axis_index("tm")
    z, x = bl // 4, bl % 4
    times, channels = 4, 1024
    rows = labels_ref.shape[1]

    loads = [
        pltpu.make_async_copy(vis_re, raw.at[0], load_sem.at[0]),
        pltpu.make_async_copy(vis_im, raw.at[1], load_sem.at[1]),
        pltpu.make_async_copy(high_hbm, table.at[0], load_sem.at[2]),
        pltpu.make_async_copy(low_hbm, table.at[1], load_sem.at[3]),
    ]
    for load in loads:
        load.start()

    def partner(offset):
        return ((z + offset[0]) % 8) * 4 + (x + offset[1]) % 4

    barrier = pltpu.get_barrier_semaphore()
    for offset in OFFSETS:
        pl.semaphore_signal(barrier, inc=1, device_id=(partner(offset), tm), device_id_type=MESH)
    for e in range(1, 8):
        pl.semaphore_signal(barrier, inc=1, device_id=(bl, (tm + e) % 8), device_id_type=MESH)

    found = index_rows(labels_ref, owner_ref, sel)
    spread = (iota((rows, 4 * rows), 1) // 4 == iota((rows, 4 * rows), 0)).astype(F32).astype(BF16)
    packed = jnp.concatenate(
        [found[0:1], weights_ref[...].astype(F32), jnp.zeros((3, rows), F32)], axis=0
    )
    wide = dot(packed.astype(BF16), spread)
    time_of = iota((1, 4 * rows), 1) % 4
    slot_wide = wide[0:1]
    weight_wide = jnp.zeros((1, 4 * rows), F32)
    for t in range(times):
        weight_wide = jnp.where(time_of == t, wide[1 + t : 2 + t], weight_wide)

    slot_iota = iota((128, 1), 0)
    slot_f = slot_iota.astype(F32)
    swapped_f = (slot_iota + 4 - 8 * ((slot_iota % 8) // 4)).astype(F32)
    lane = iota((128, 128), 1)
    row = iota((128, 128), 0)
    rank_col = jnp.max(jnp.where(found[0:1] == slot_f, found[1:2], 0.0), axis=1, keepdims=True)
    by_slot = jnp.where(lane == (row % 4) * 32, rank_col, 0.0)
    scale_even = jnp.zeros((128, 128), F32)
    scale_odd = jnp.zeros((128, 128), F32)

    loads[0].wait()
    loads[1].wait()
    for part in range(2):
        for j in range(4):
            flat[:, part * channels + 256 * j : part * channels + 256 * j + 256] = raw[
                part, :, :, 256 * j : 256 * j + 256
            ].reshape(4 * rows, 256)

    def send_chunk(t):
        for i, offset in enumerate(OFFSETS):
            to = partner(offset)
            pltpu.make_async_remote_copy(
                src_ref=sent.at[t, to % 2, to // 2],
                dst_ref=held.at[t, i + 1],
                send_sem=send_sem.at[t],
                recv_sem=recv_sem.at[t],
                device_id=(to, tm),
                device_id_type=MESH,
            ).start()

    top = (iota((128, 1), 0) % 8) < 4
    for t in range(times):
        slot_t = jnp.where(time_of == t, slot_wide, -1.0)
        fold_re = jnp.where(slot_t == slot_f, weight_wide, 0.0)
        fold_im = jnp.where(slot_t == swapped_f, weight_wide, 0.0)
        weight_col = jnp.sum(fold_re, axis=1, keepdims=True)
        by_slot = jnp.where(lane == (row % 4) * 32 + 1 + t, weight_col, by_slot)
        re = dot(fold_re.astype(BF16), flat[:, :channels])
        im = dot(fold_im.astype(BF16), flat[:, channels:])
        scales = []
        for parity in range(2):
            piece = jnp.where(top, re, im) if parity == 0 else jnp.where(top, im, re)
            largest = jnp.max(jnp.abs(piece), axis=1, keepdims=True)
            scale = jnp.maximum(largest, 1e-30) * (1.0079 / 32767.0)
            scale = scale.astype(BF16).astype(F32)
            scales.append(scale)
            code = jnp.round(piece * (1.0 / scale)).astype(I32)
            both = jnp.bitwise_or(
                jnp.left_shift(code[:, 512:], 16), jnp.bitwise_and(code[:, :512], 0xFFFF)
            )
            sent[t, parity] = both.reshape(16, 8, 512)
        here = lane == (row % 4) * 32 + 5 + 4 * ((row % 8) // 4) + t
        scale_even = jnp.where(here, scales[0], scale_even)
        scale_odd = jnp.where(here, scales[1], scale_odd)
        if t == times - 1:
            owner32, row32 = iota((32, 128), 0), iota((32, 128), 1)
            meta = (
                dot((row32 // 4 == owner32).astype(F32).astype(BF16), by_slot.astype(BF16))
                + dot((2 * (row32 // 8) == owner32).astype(F32).astype(BF16), scale_even.astype(BF16))
                + dot((2 * (row32 // 8) + 1 == owner32).astype(F32).astype(BF16), scale_odd.astype(BF16))
            )
            for o in range(32):
                meta_out[o] = meta[o : o + 1]
        if t == 0:
            pl.semaphore_wait(barrier, 38)
        if t == times - 1:
            for i, offset in enumerate(OFFSETS):
                to = partner(offset)
                pltpu.make_async_remote_copy(
                    src_ref=meta_out.at[to],
                    dst_ref=meta_in.at[i + 1],
                    send_sem=meta_send,
                    recv_sem=meta_recv,
                    device_id=(to, tm),
                    device_id_type=MESH,
                ).start()
        send_chunk(t)
        held[t, 0] = sent[t, bl % 2, bl // 2]
    meta_in[0] = meta_out[bl]

    loads[2].wait()
    loads[3].wait()
    pltpu.make_async_copy(meta_in.at[pl.ds(1, 31)], meta_in.at[pl.ds(1, 31)], meta_recv).wait()
    meta = jnp.concatenate([meta_in[i] for i in range(32)], axis=0)
    held_row, held_lane = iota((256, 128), 0), iota((256, 128), 1)
    expand = (iota((256, 32), 0) // 8 == iota((256, 32), 1)).astype(F32).astype(BF16)
    info = dot(expand, meta.astype(BF16))
    base = (held_row % 4) * 32
    flip = bl % 2

    def column(k):
        return jnp.sum(jnp.where(held_lane == base + k, info, 0.0), axis=1, keepdims=True)

    quadrant = jnp.where(flip == 0, (held_row % 8) // 4, 1 - (held_row % 8) // 4)
    chooser = jnp.where(
        jnp.logical_and(
            column(0) == (held_lane % 64).astype(F32), quadrant == held_lane // 64
        ),
        1.0,
        0.0,
    )
    chooser = jnp.transpose(chooser).astype(BF16)
    scale_cols, weight_mat = [], jnp.zeros((256, 128), F32)
    for t in range(times):
        scale_cols.append(column(5 + 4 * ((held_row % 8) // 4) + t))
        weight_mat = jnp.where(held_lane == t, column(1 + t), weight_mat)
    weight_sum = dot(chooser, weight_mat.astype(BF16))
    inverse = 1.0 / jnp.maximum(weight_sum, 1.0)

    cosine = [twiddle_ref[k : k + 1] for k in range(4)]
    sine = [twiddle_ref[4 + k : 5 + k] for k in range(4)]

    def spectrum(t):
        both = held[t].reshape(256, 512)
        low_part = jnp.right_shift(jnp.left_shift(both, 16), 16)
        high_part = jnp.right_shift(both, 16)
        arrived = jnp.concatenate([low_part, high_part], axis=1).astype(F32) * scale_cols[t]
        coarse = arrived.astype(BF16)
        fine = (arrived - coarse.astype(F32)).astype(BF16)
        total = dot(chooser, coarse) + dot(chooser, fine)
        mean = total * (inverse[:, t : t + 1] * taper_ref[...])
        xr = [mean[:64, 256 * j : 256 * j + 256] for j in range(4)]
        xi = [mean[64:, 256 * j : 256 * j + 256] for j in range(4)]
        ar, ai, cr, ci = xr[0] + xr[2], xi[0] + xi[2], xr[0] - xr[2], xi[0] - xi[2]
        br, bi, dr, di = xr[1] + xr[3], xi[1] + xi[3], xr[1] - xr[3], xi[1] - xi[3]
        yr = [ar + br, cr + di, ar - br, cr - di]
        yi = [ai + bi, ci - dr, ai - bi, ci + dr]
        stacked = []
        for k in range(4):
            re, im = yr[k], yi[k]
            if k:
                re, im = re * cosine[k] + im * sine[k], im * cosine[k] - re * sine[k]
            stacked.append(jnp.concatenate([re, im], axis=1))
        y = jnp.concatenate(stacked, axis=0)
        y_high = y.astype(BF16)
        y_low = (y - y_high.astype(F32)).astype(BF16)
        return dot(y_high, table[0]) + dot(y_low, table[0]) + dot(y_high, table[1])

    edge = pltpu.make_async_remote_copy(
        src_ref=first,
        dst_ref=after,
        send_sem=edge_send,
        recv_sem=edge_recv,
        device_id=(bl, (tm + 7) % 8),
        device_id_type=MESH,
    )
    power = None
    previous = None
    for t in range(times):
        pltpu.make_async_copy(
            held.at[t, pl.ds(1, 31)], held.at[t, pl.ds(1, 31)], recv_sem.at[t]
        ).wait()
        now = spectrum(t)
        if t == 0:
            first[...] = now
            edge.start()
        elif t == 1:
            power = previous * now
        else:
            power = power + previous * now
        previous = now
    edge.wait()
    power = power + jnp.where(tm < 7, previous * after[...], 0.0)
    power = power[:, :256] + power[:, 256:]
    for m in range(8):
        for k in range(4):
            parts[m, k] = power[64 * k + 8 * m : 64 * k + 8 * m + 8]
    for e in range(1, 8):
        to = (tm + e) % 8
        pltpu.make_async_remote_copy(
            src_ref=parts.at[to],
            dst_ref=fb.at[e],
            send_sem=part_send,
            recv_sem=part_recv,
            device_id=(bl, to),
            device_id_type=MESH,
        ).start()
    fb[0] = parts[tm]

    for t in range(times):
        pltpu.make_async_copy(
            held.at[t, pl.ds(1, 31)], held.at[t, pl.ds(1, 31)], send_sem.at[t]
        ).wait()
    pltpu.make_async_copy(meta_in.at[pl.ds(1, 31)], meta_in.at[pl.ds(1, 31)], meta_send).wait()
    pltpu.make_async_copy(fb.at[pl.ds(1, 7)], fb.at[pl.ds(1, 7)], part_send).wait()
    pltpu.make_async_copy(fb.at[pl.ds(1, 7)], fb.at[pl.ds(1, 7)], part_recv).wait()
    summed = fb[0]
    for e in range(1, 8):
        summed = summed + fb[e]
    out_ref[...] = summed


def interleave(x_ref, o_ref):
    lane = iota((8, 128), 1)
    for b in range(8):
        value = jnp.zeros((8, 128), F32)
        for k in range(4):
            source = x_ref[k, :, 128 * (b // 4) : 128 * (b // 4) + 128]
            taken = jnp.take_along_axis(source, 32 * (b % 4) + lane // 4, axis=1)
            value = jnp.where(lane % 4 == k, taken, value)
        o_ref[:, 128 * b : 128 * b + 128] = value


def per_device(visibility_real, visibility_imag, weights, labels, owner_of):
    rows, times, channels = visibility_real.shape
    high, low, twiddle = dft_constants(channels)
    taper = taper_row(channels)
    vmem = pl.BlockSpec(memory_space=pltpu.VMEM)
    hbm = pl.BlockSpec(memory_space=pl.ANY)
    dma = pltpu.SemaphoreType.DMA
    summed = pl.pallas_call(
        kernel,
        out_shape=jax.ShapeDtypeStruct((4, 8, 256), F32),
        in_specs=[vmem] * 5 + [hbm] * 4,
        out_specs=vmem,
        scratch_shapes=[
            pltpu.VMEM((2, rows, times, channels), BF16),
            pltpu.VMEM((rows * times, 2 * channels), BF16),
            pltpu.VMEM((rows, owner_of.shape[0]), BF16),
            pltpu.VMEM((times, 2, 16, 8, 512), I32),
            pltpu.VMEM((times, 32, 8, 512), I32),
            pltpu.VMEM((32, 1, 128), F32),
            pltpu.VMEM((32, 1, 128), F32),
            pltpu.VMEM((2, 512, 512), BF16),
            pltpu.VMEM((256, 512), F32),
            pltpu.VMEM((256, 512), F32),
            pltpu.VMEM((8, 4, 8, 256), F32),
            pltpu.VMEM((8, 4, 8, 256), F32),
            dma((4,)),
            dma((4,)),
            dma((4,)),
            dma(()),
            dma(()),
            dma(()),
            dma(()),
            dma(()),
            dma(()),
        ],
        compiler_params=pltpu.CompilerParams(
            collective_id=0, has_side_effects=True, vmem_limit_bytes=60 * 1024 * 1024
        ),
        name="bandpower",
    )(
        labels.reshape(1, rows), owner_of.reshape(1, -1), weights.T, jnp.asarray(taper),
        jnp.asarray(twiddle), visibility_real, visibility_imag, jnp.asarray(high), jnp.asarray(low),
    )
    return pl.pallas_call(
        interleave,
        out_shape=jax.ShapeDtypeStruct((8, channels), F32),
        in_specs=[vmem],
        out_specs=vmem,
        name="interleave",
    )(summed)


def solution(mesh):
    placed = (P("bl", "tm", None), P("bl", "tm", None), P("bl", "tm"), P("bl"), P())
    return jax.shard_map(
        per_device, mesh=mesh, in_specs=placed, out_specs=P(("bl", "tm"), None), check_vma=False
    )
```

time: 222 us -> 71.8 us (0.32)
  Pallas kernels: 0 us -> 70.3 us
  waiting for transfers between devices: 66.1 us -> 0 us
  other arithmetic: 44.2 us -> 0 us
  starting transfers between devices: 40.7 us -> 0 us
  matrix products: 29.5 us -> 0 us
  local copies, waits for them, and re-layouts: 28.3 us -> 1.24 us
  blocking collectives: 10.5 us -> 0 us
    pallas_call x0 -> x2, Pallas kernels: none -> 70.3 us  [the longest x1 68.8 us: per_device(): pl.pallas_call(kernel, out_shape=jax.ShapeDtypeStruct((4, 8, 256), F32),...]
    all_to_all x4 -> x0, waiting for transfers between devices: 58.3 us -> none  [the longest x1 34.7 us: per_device(): lax.all_to_all(part_real, 'bl', split_axis=0, concat_axis=0, tiled=True)]
    all_to_all x4 -> x0, starting transfers between devices: 32.8 us -> none  [the longest x1 11.9 us: per_device(): lax.all_to_all(send_rank, 'bl', split_axis=0, concat_axis=0, tiled=True)]
    dot_general x6 -> x0, matrix products: 29.5 us -> none  [the longest x1 8.23 us: per_device(): jnp.einsum('gnf,fk->gnk', mean_real, table_real, precision=lax.Precision....]
    mul x2 -> x0, other arithmetic: 19.6 us -> none  [the longest x1 19.6 us: dft_tables(): sine_part = jnp.sin(phase_angle) * window_taper[:, None]]
    reshape x6 -> x1, local copies, waits for them, and re-layouts: 17.9 us -> 1.24 us  [per_device(): labels.reshape(1, rows)]
    another operation x4 -> x0, other arithmetic: 16.5 us -> none
    all_to_all x1 -> x0, blocking collectives: 10.5 us -> none  [summed_on_arrival(): blocks = lax.all_to_all(in_blocks(x, dim, size), axis, 0, 0, tiled=True)]
  transfers between devices with their start and end apart: 5 -> 0, of which waited for: 4 -> 0; matrix products, arithmetic and copies ran while one was open for 23% -> 0% of each run, Pallas kernels for 0% -> 0%
where the time goes in v1:
time: 71.8 us; the launch traced here: 71.6 us
  Pallas kernels  70.3 us (98%)
  local copies, waits for them, and re-layouts  1.24 us (2%)
    pallas_call x1, Pallas kernels, per_device(): pl.pallas_call(kernel, out_shape=jax.ShapeDtypeStruct((4, 8, 256), F32),...  68.8 us
    pallas_call x1, Pallas kernels, per_device(): pl.pallas_call(interleave, out_shape=jax.ShapeDtypeStruct((8, channels),...  1.52 us

profile of v1, /device:TPU:1, one launch (start us, length us, event | category | flops | bytes accessed | tf_op | source)
XLA Modules:
  0.0 71.6 jit_solution(18119576137267127507)
XLA Ops:
  0.0 1.2 %reshape.6.labels_ref = s32[1,384]{1,0:T(1,128)} reshape(s32[384]{0:T(512)} %param.12) | data formatting | bytes 3072 | tf_op jit(solution)/shard_map/reshape | solution.py:376
  1.2 68.8 %bandpower.1.x_ref = f32[4,8,256]{2,1,0:T(8,128)} custom-call(s32[1,384]{1,0:T(1,128)} %reshape.6.labels_ref, s32[1,2048]{1,0:T(1,128)} %bitcast.2, s32[4,384]{1,0:T(4,128)} %bitcast.3, f32[1,1024]{1,0:T(1,128)} %constant.8.clone.taper_ref, f32[8,256]{1,0:T(8,128)} %constant.9.clone.twiddle_ref, bf16[384,4,1024]{2,1,0:T(4,128)(2,1)} %vis_re.1, ...), custom_call_target="tpu_custom_call" | custom-call | tf_op jit(solution)/shard_map/bandpower/pallas_call | solution.py:343
  70.1 1.5 %interleave.1 = f32[8,1024]{1,0:T(8,128)} custom-call(f32[4,8,256]{2,1,0:T(8,128)} %bandpower.1.x_ref), custom_call_target="tpu_custom_call" | custom-call | tf_op jit(solution)/shard_map/interleave/pallas_call | solution.py:379

commit v2 on v1

v2 whole, which is shorter than its diff:
```python
import functools
import math

import jax
import jax.numpy as jnp
import numpy as np
from jax import lax
from jax.experimental import pallas as pl
from jax.experimental.pallas import tpu as pltpu
from jax.sharding import PartitionSpec as P

HARRIS = (0.35875, 0.48829, 0.14128, 0.01168)
MESH = pl.DeviceIdType.MESH
F32, BF16, I32 = jnp.float32, jnp.bfloat16, jnp.int32

OFFSETS = [
    (dz, dx) for dx in (0, 1, 2, 3) for dz in (1, 7, 2, 6, 3, 5, 4, 0) if (dz, dx) != (0, 0)
]


def taper_row(length):
    angle = 2.0 * np.pi / length * np.arange(length)
    h = (
        HARRIS[0]
        - HARRIS[1] * np.cos(angle)
        + HARRIS[2] * np.cos(2.0 * angle)
        - HARRIS[3] * np.cos(3.0 * angle)
    )
    return (h / np.sqrt(np.sum(h * h)))[None, :].astype(np.float32)


def dft_constants(length):
    n = length // 4
    angle = 2.0 * np.pi / n * (np.outer(np.arange(n), np.arange(n)) % n)
    c, s = np.cos(angle), np.sin(angle)
    table = np.block([[c, -s], [s, c]]).astype(np.float32)
    high = table.astype(jnp.bfloat16)
    low = (table - high.astype(np.float32)).astype(jnp.bfloat16)
    turn = 2.0 * np.pi / length * np.outer(np.arange(4), np.arange(n))
    twiddle = np.concatenate([np.cos(turn), np.sin(turn)], axis=0).astype(np.float32)
    return high, low, twiddle


def iota(shape, dim):
    return lax.broadcasted_iota(I32, shape, dim)


def dot(a, b):
    return jnp.dot(a, b, preferred_element_type=F32)


def dot_t(a, b):
    return lax.dot_general(a, b, (((1,), (1,)), ((), ())), preferred_element_type=F32)


def index_rows(labels_ref, owner_ref):
    rows = labels_ref.shape[0]
    blocks = owner_ref.shape[0]
    labels = labels_ref[...].reshape(1, rows)
    high = (labels // 128 == iota((blocks, rows), 0)).astype(F32)
    low = (labels % 128 == iota((128, rows), 0)).astype(F32).astype(BF16)
    present = dot_t(high.astype(BF16), low)
    present = jnp.where(present > 0.0, 1.0, 0.0)
    owner_iota = iota((32, 128), 0)
    hits, marks = [], []
    for b in range(blocks):
        hit = (owner_ref[b : b + 1, :] == owner_iota).astype(F32)
        hits.append(hit)
        marks.append(hit)
        marks.append(hit * present[b : b + 1])
    stacked = jnp.concatenate(marks, axis=0).astype(BF16)
    earlier = jnp.logical_or(iota((128, 256), 0) < iota((128, 256), 1), iota((128, 256), 1) >= 128)
    sums = dot(stacked, earlier.astype(F32).astype(BF16))
    before = jnp.zeros((64, 128), F32)
    ranks, slots = [], []
    for b in range(blocks):
        within = sums[64 * b : 64 * b + 64]
        prefix = within[:, :128] + before
        before = before + within[:, 128:]
        ranks.append(jnp.sum(hits[b] * prefix[:32], axis=0, keepdims=True))
        first_slot = 4.0 * owner_iota.astype(F32)
        slots.append(jnp.sum(hits[b] * (prefix[32:] + first_slot), axis=0, keepdims=True))
    table = jnp.concatenate(slots + ranks, axis=0).astype(BF16)
    found = dot(table, low)
    slot = jnp.sum(high * found[:blocks], axis=0, keepdims=True)
    rank = jnp.sum(high * found[blocks:], axis=0, keepdims=True)
    return slot, rank


def kernel(
    labels_hbm, owner_hbm, weights_hbm, taper_hbm, twiddle_hbm, vis_re, vis_im, high_hbm, low_hbm,
    out_ref,
    labels_ref, owner_ref, weights_ref, taper_ref, twiddle_ref, raw, sums, sent, held,
    meta_out, meta_in, table, first, after, parts, fb,
    load_sem, send_sem, recv_sem, meta_send, meta_recv, edge_send, edge_recv, part_send, part_recv,
):
    bl, tm = lax.axis_index("bl"), lax.axis_index("tm")
    z, x = bl // 4, bl % 4
    times, channels = 4, 1024
    rows = labels_ref.shape[0]

    pairs = [
        (labels_hbm, labels_ref),
        (owner_hbm, owner_ref),
        (weights_hbm, weights_ref),
        (taper_hbm, taper_ref),
        (twiddle_hbm, twiddle_ref),
        (vis_re, raw.at[0]),
        (vis_im, raw.at[1]),
        (high_hbm, table.at[0]),
        (low_hbm, table.at[1]),
    ]
    loads = [
        pltpu.make_async_copy(source, target, load_sem.at[n])
        for n, (source, target) in enumerate(pairs)
    ]
    for load in loads:
        load.start()

    def partner(offset):
        return ((z + offset[0]) % 8) * 4 + (x + offset[1]) % 4

    barrier = pltpu.get_barrier_semaphore()
    for offset in OFFSETS:
        pl.semaphore_signal(barrier, inc=1, device_id=(partner(offset), tm), device_id_type=MESH)
    for e in range(1, 8):
        pl.semaphore_signal(barrier, inc=1, device_id=(bl, (tm + e) % 8), device_id_type=MESH)

    for n in range(5):
        loads[n].wait()
    slot_row, rank_row = index_rows(labels_ref, owner_ref)
    spread = (iota((rows, 4 * rows), 1) // 4 == iota((rows, 4 * rows), 0)).astype(F32).astype(BF16)
    packed = jnp.concatenate(
        [slot_row, weights_ref[...].astype(F32), jnp.zeros((3, rows), F32)], axis=0
    )
    wide = dot(packed.astype(BF16), spread)
    time_of = iota((1, 4 * rows), 1) % 4
    slot_wide = wide[0:1]
    weight_wide = jnp.zeros((1, 4 * rows), F32)
    for t in range(times):
        weight_wide = jnp.where(time_of == t, wide[1 + t : 2 + t], weight_wide)

    slot_f = iota((128, 1), 0).astype(F32)
    lane = iota((128, 256), 1)
    row = iota((128, 256), 0)
    by_slot = None
    scale_even = jnp.zeros((128, 256), F32)
    scale_odd = jnp.zeros((128, 256), F32)

    cosine = [twiddle_ref[k : k + 1] for k in range(4)]
    sine = [twiddle_ref[4 + k : 5 + k] for k in range(4)]
    top = (iota((128, 1), 0) % 8) < 4

    def send_chunk(h, t):
        for i, offset in enumerate(OFFSETS):
            to = partner(offset)
            pltpu.make_async_remote_copy(
                src_ref=sent.at[h, t, to % 2, to // 2],
                dst_ref=held.at[h, t, i + 1],
                send_sem=send_sem.at[h, t],
                recv_sem=recv_sem.at[h, t],
                device_id=(to, tm),
                device_id_type=MESH,
            ).start()

    def spectra(q, xr, xi):
        if q % 2 == 0:
            ar, ai, br, bi = xr[0] + xr[2], xi[0] + xi[2], xr[1] + xr[3], xi[1] + xi[3]
        else:
            ar, ai, br, bi = xr[0] - xr[2], xi[0] - xi[2], xi[1] - xi[3], xr[3] - xr[1]
        re, im = (ar + br, ai + bi) if q < 2 else (ar - br, ai - bi)
        if q:
            re, im = re * cosine[q] + im * sine[q], im * cosine[q] - re * sine[q]
        y = jnp.concatenate([re, im], axis=1)
        y_high = y.astype(BF16)
        y_low = (y - y_high.astype(F32)).astype(BF16)
        out = dot(y_high, table[0]) + dot(y_low, table[0]) + dot(y_high, table[1])
        return out[:, :256], out[:, 256:]

    folds = [
        jnp.where(jnp.where(time_of == t, slot_wide, -1.0) == slot_f, weight_wide, 0.0)
        for t in range(times)
    ]

    def fold_sums(fold):
        fold = fold.astype(BF16)
        both = []
        for part in range(2):
            if fold.shape[0] == 128:
                loads[5 + part].wait()
            blocks = [
                dot(fold, raw[part, :, :, 256 * j : 256 * j + 256].reshape(4 * rows, 256))
                for j in range(4)
            ]
            both.append(jnp.concatenate(blocks, axis=1) * taper_ref[...])
        return both

    for t in range(times):
        weight_col = jnp.sum(folds[t], axis=1, keepdims=True)
        if t == 0:
            re, im = fold_sums(folds[0])
        else:
            if t == 1:
                sums[0], sums[1] = fold_sums(jnp.concatenate(folds[1:], axis=0))
            re = sums[0, 128 * t - 128 : 128 * t]
            im = sums[1, 128 * t - 128 : 128 * t]
        xr = [re[:, 256 * j : 256 * j + 256] for j in range(4)]
        xi = [im[:, 256 * j : 256 * j + 256] for j in range(4)]
        if t == 0:
            loads[7].wait()
            loads[8].wait()
        for h in range(4):
            real, imag = spectra(h, xr, xi)
            imag = pltpu.roll(imag.reshape(16, 8, 256), 4, 1).reshape(128, 256)
            scales = []
            for parity in range(2):
                piece = jnp.where(top, real, imag) if parity == 0 else jnp.where(top, imag, real)
                largest = jnp.max(jnp.abs(piece), axis=1, keepdims=True)
                scale = jnp.maximum(largest, 1e-30) * (1.0079 / 32767.0)
                scale = scale.astype(BF16).astype(F32)
                scales.append(scale)
                code = jnp.round(piece * (1.0 / scale)).astype(I32)
                both = jnp.bitwise_or(
                    jnp.left_shift(code[:, 128:], 16), jnp.bitwise_and(code[:, :128], 0xFFFF)
                )
                sent[h, t, parity] = both.reshape(16, 8, 128)
            if h == 0 and t == 0:
                pl.semaphore_wait(barrier, 38)
            if h < 2:
                send_chunk(h, t)
            here = lane == (row % 4) * 64 + 5 + 8 * h + 4 * ((row % 8) // 4) + t
            scale_even = jnp.where(here, scales[0], scale_even)
            scale_odd = jnp.where(here, scales[1], scale_odd)
        if t == 0:
            rank_col = jnp.max(
                jnp.where(slot_row == slot_f, rank_row, 0.0), axis=1, keepdims=True
            )
            by_slot = jnp.where(lane == (row % 4) * 64, rank_col, 0.0)
        by_slot = jnp.where(lane == (row % 4) * 64 + 1 + t, weight_col, by_slot)

    owner32, row32 = iota((32, 128), 0), iota((32, 128), 1)
    meta = (
        dot((row32 // 4 == owner32).astype(F32).astype(BF16), by_slot.astype(BF16))
        + dot((2 * (row32 // 8) == owner32).astype(F32).astype(BF16), scale_even.astype(BF16))
        + dot((2 * (row32 // 8) + 1 == owner32).astype(F32).astype(BF16), scale_odd.astype(BF16))
    )
    for o in range(32):
        meta_out[o] = meta[o : o + 1]
    for i, offset in enumerate(OFFSETS):
        to = partner(offset)
        pltpu.make_async_remote_copy(
            src_ref=meta_out.at[to],
            dst_ref=meta_in.at[i + 1],
            send_sem=meta_send,
            recv_sem=meta_recv,
            device_id=(to, tm),
            device_id_type=MESH,
        ).start()
    for h in range(2, 4):
        for t in range(times):
            send_chunk(h, t)
    meta_in[0] = meta_out[bl]
    for h in range(4):
        for t in range(times):
            held[h, t, 0] = sent[h, t, bl % 2, bl // 2]

    pltpu.make_async_copy(meta_in.at[pl.ds(1, 31)], meta_in.at[pl.ds(1, 31)], meta_recv).wait()
    meta = jnp.concatenate([meta_in[i] for i in range(32)], axis=0)
    held_row, held_lane = iota((256, 128), 0), iota((256, 128), 1)
    expand = (iota((256, 32), 0) // 8 == iota((256, 32), 1)).astype(F32).astype(BF16)
    info = dot(expand, meta.astype(BF16))
    info = jnp.where(held_row % 4 < 2, info[:, :128], info[:, 128:])
    base = (held_row % 2) * 64
    flip = bl % 2

    def column(k):
        return jnp.sum(jnp.where(held_lane == base + k, info, 0.0), axis=1, keepdims=True)

    quadrant = jnp.where(flip == 0, (held_row % 8) // 4, 1 - (held_row % 8) // 4)
    chooser = jnp.where(
        jnp.logical_and(
            column(0) == (held_lane % 64).astype(F32), quadrant == held_lane // 64
        ),
        1.0,
        0.0,
    )
    chooser = jnp.transpose(chooser).astype(BF16)
    weight_mat = jnp.zeros((256, 128), F32)
    for t in range(times):
        weight_mat = jnp.where(held_lane == t, column(1 + t), weight_mat)
    weight_sum = dot(chooser, weight_mat.astype(BF16))
    inverse = 1.0 / jnp.maximum(weight_sum, 1.0)

    def edge(h):
        return pltpu.make_async_remote_copy(
            src_ref=first.at[h],
            dst_ref=after.at[h],
            send_sem=edge_send.at[h],
            recv_sem=edge_recv.at[h],
            device_id=(bl, (tm + 7) % 8),
            device_id_type=MESH,
        )

    for h in range(4):
        power, previous = None, None
        for t in range(times):
            scale_col = column(5 + 8 * h + 4 * ((held_row % 8) // 4) + t)
            pltpu.make_async_copy(
                held.at[h, t, pl.ds(1, 31)], held.at[h, t, pl.ds(1, 31)], recv_sem.at[h, t]
            ).wait()
            both = held[h, t].reshape(256, 128)
            low_part = jnp.right_shift(jnp.left_shift(both, 16), 16)
            high_part = jnp.right_shift(both, 16)
            arrived = jnp.concatenate([low_part, high_part], axis=1).astype(F32) * scale_col
            coarse = arrived.astype(BF16)
            fine = (arrived - coarse.astype(F32)).astype(BF16)
            now = (dot(chooser, coarse) + dot(chooser, fine)) * inverse[:, t : t + 1]
            if t == 0:
                first[h] = now
                edge(h).start()
            elif t == 1:
                power = previous * now
            else:
                power = power + previous * now
            previous = now
        edge(h).wait()
        power = power + jnp.where(tm < 7, previous * after[h], 0.0)
        parts[h] = (power[:64] + power[64:]).reshape(8, 8, 256)
        for e in range(1, 8):
            to = (tm + e) % 8
            pltpu.make_async_remote_copy(
                src_ref=parts.at[h, to],
                dst_ref=fb.at[h, e],
                send_sem=part_send.at[h],
                recv_sem=part_recv.at[h],
                device_id=(bl, to),
                device_id_type=MESH,
            ).start()
        fb[h, 0] = parts[h, tm]

    for h in range(4):
        for t in range(times):
            pltpu.make_async_copy(
                held.at[h, t, pl.ds(1, 31)], held.at[h, t, pl.ds(1, 31)], send_sem.at[h, t]
            ).wait()
    pltpu.make_async_copy(meta_in.at[pl.ds(1, 31)], meta_in.at[pl.ds(1, 31)], meta_send).wait()
    for h in range(4):
        arrivals = fb.at[h, pl.ds(1, 7)]
        pltpu.make_async_copy(arrivals, arrivals, part_send.at[h]).wait()
        pltpu.make_async_copy(arrivals, arrivals, part_recv.at[h]).wait()
        summed = fb[h, 0]
        for e in range(1, 8):
            summed = summed + fb[h, e]
        out_ref[h] = summed


def interleave(x_ref, o_ref):
    lane = iota((8, 128), 1)
    for b in range(8):
        value = jnp.zeros((8, 128), F32)
        for k in range(4):
            source = x_ref[k, :, 128 * (b // 4) : 128 * (b // 4) + 128]
            taken = jnp.take_along_axis(source, 32 * (b % 4) + lane // 4, axis=1)
            value = jnp.where(lane % 4 == k, taken, value)
        o_ref[:, 128 * b : 128 * b + 128] = value


def per_device(visibility_real, visibility_imag, weights, labels, owner_of):
    rows, times, channels = visibility_real.shape
    high, low, twiddle = dft_constants(channels)
    taper = taper_row(channels)
    vmem = pl.BlockSpec(memory_space=pltpu.VMEM)
    hbm = pl.BlockSpec(memory_space=pl.ANY)
    dma = pltpu.SemaphoreType.DMA
    summed = pl.pallas_call(
        kernel,
        out_shape=pltpu.VMEM((4, 8, 256), F32),
        in_specs=[hbm] * 9,
        out_specs=vmem,
        scratch_shapes=[
            pltpu.VMEM((rows,), I32),
            pltpu.VMEM((owner_of.shape[0] // 128, 128), I32),
            pltpu.VMEM((times, rows), I32),
            pltpu.VMEM((1, channels), F32),
            pltpu.VMEM((8, channels // 4), F32),
            pltpu.VMEM((2, rows, times, channels), BF16),
            pltpu.VMEM((2, rows, channels), F32),
            pltpu.VMEM((4, times, 2, 16, 8, 128), I32),
            pltpu.VMEM((4, times, 32, 8, 128), I32),
            pltpu.VMEM((32, 1, 256), F32),
            pltpu.VMEM((32, 1, 256), F32),
            pltpu.VMEM((2, 512, 512), BF16),
            pltpu.VMEM((4, 128, 256), F32),
            pltpu.VMEM((4, 128, 256), F32),
            pltpu.VMEM((4, 8, 8, 256), F32),
            pltpu.VMEM((4, 8, 8, 256), F32),
            dma((9,)),
            dma((4, times)),
            dma((4, times)),
            dma(()),
            dma(()),
            dma((4,)),
            dma((4,)),
            dma((4,)),
            dma((4,)),
        ],
        compiler_params=pltpu.CompilerParams(
            collective_id=0, has_side_effects=True, vmem_limit_bytes=60 * 1024 * 1024
        ),
        name="bandpower",
    )(
        labels, owner_of.reshape(-1, 128), weights.T, jnp.asarray(taper),
        jnp.asarray(twiddle), visibility_real, visibility_imag, jnp.asarray(high), jnp.asarray(low),
    )
    return pl.pallas_call(
        interleave,
        out_shape=jax.ShapeDtypeStruct((8, channels), F32),
        in_specs=[vmem],
        out_specs=vmem,
        name="interleave",
    )(pltpu.with_memory_space_constraint(summed, pltpu.VMEM))


def solution(mesh):
    placed = (P("bl", "tm", None), P("bl", "tm", None), P("bl", "tm"), P("bl"), P())
    return jax.shard_map(
        per_device, mesh=mesh, in_specs=placed, out_specs=P(("bl", "tm"), None), check_vma=False
    )
```

time: 71.8 us -> 66.9 us (0.932)
  Pallas kernels: 70.3 us -> 66.8 us
  local copies, waits for them, and re-layouts: 1.24 us -> 0 us
    pallas_call x1, Pallas kernels: 68.8 us -> 66 us  [per_device(): pl.pallas_call(kernel, out_shape=pltpu.VMEM((4, 8, 256), F32), in_specs=[...]
    reshape x1 -> x0, local copies, waits for them, and re-layouts: 1.24 us -> none  [per_device(): labels.reshape(1, rows)]
    pallas_call x1, Pallas kernels: 1.52 us -> 0.76 us  [per_device(): pl.pallas_call(interleave, out_shape=jax.ShapeDtypeStruct((8, channels),...]
where the time goes in v2:
time: 66.9 us; the launch traced here: 66.8 us
  Pallas kernels  66.8 us (100%)
    pallas_call x1, Pallas kernels, per_device(): pl.pallas_call(kernel, out_shape=pltpu.VMEM((4, 8, 256), F32), in_specs=[...  66 us

profile of v2, /device:TPU:1, one launch (start us, length us, event | category | flops | bytes accessed | tf_op | source)
XLA Modules:
  0.0 66.8 jit_solution(1367393028578304439)
XLA Ops:
  0.0 66.0 %bandpower.1.x_ref = f32[4,8,256]{2,1,0:T(8,128)S(1)} custom-call(s32[384]{0:T(512)} %labels_hbm.1, s32[16,128]{1,0:T(8,128)} %bitcast.2, s32[4,384]{1,0:T(4,128)} %bitcast.3, f32[1,1024]{1,0:T(1,128)} %constant.8.clone.taper_hbm, f32[8,256]{1,0:T(8,128)} %constant.9.clone.twiddle_hbm, bf16[384,4,1024]{2,1,0:T(4,128)(2,1)} %vis_re.1, ...), custom_call_target="tpu_custom_call" | custom-call | tf_op jit(solution)/shard_map/bandpower/pallas_call | solution.py:375
  66.0 0.8 %interleave.1 = f32[8,1024]{1,0:T(8,128)} custom-call(f32[4,8,256]{2,1,0:T(8,128)S(1)} %bandpower.1.x_ref), custom_call_target="tpu_custom_call" | custom-call | tf_op jit(solution)/shard_map/interleave/pallas_call | solution.py:415

commit v3 on v2

--- a/solution.py
+++ b/solution.py
@@ -14,7 +14,7 @@
 F32, BF16, I32 = jnp.float32, jnp.bfloat16, jnp.int32
 
 OFFSETS = [
-    (dz, dx) for dx in (0, 1, 2, 3) for dz in (1, 7, 2, 6, 3, 5, 4, 0) if (dz, dx) != (0, 0)
+    (dz, dx) for dx in (2, 1, 3, 0) for dz in (4, 3, 5, 2, 6, 1, 7, 0) if (dz, dx) != (0, 0)
 ]
 
 
@@ -141,11 +141,10 @@
         weight_wide = jnp.where(time_of == t, wide[1 + t : 2 + t], weight_wide)
 
     slot_f = iota((128, 1), 0).astype(F32)
-    lane = iota((128, 256), 1)
-    row = iota((128, 256), 0)
+    lane = iota((128, 128), 1)
+    row = iota((128, 128), 0)
     by_slot = None
-    scale_even = jnp.zeros((128, 256), F32)
-    scale_odd = jnp.zeros((128, 256), F32)
+    scales = jnp.zeros((128, 128), F32)
 
     cosine = [twiddle_ref[k : k + 1] for k in range(4)]
     sine = [twiddle_ref[4 + k : 5 + k] for k in range(4)]
@@ -162,6 +161,12 @@
                 device_id=(to, tm),
                 device_id_type=MESH,
             ).start()
+
+    def coded(value, inverse_scale):
+        code = jnp.round(value * inverse_scale).astype(I32)
+        return jnp.bitwise_or(
+            jnp.left_shift(code[:, 128:], 16), jnp.bitwise_and(code[:, :128], 0xFFFF)
+        )
 
     def spectra(q, xr, xi):
         if q % 2 == 0:
@@ -211,39 +216,31 @@
             loads[8].wait()
         for h in range(4):
             real, imag = spectra(h, xr, xi)
-            imag = pltpu.roll(imag.reshape(16, 8, 256), 4, 1).reshape(128, 256)
-            scales = []
-            for parity in range(2):
-                piece = jnp.where(top, real, imag) if parity == 0 else jnp.where(top, imag, real)
-                largest = jnp.max(jnp.abs(piece), axis=1, keepdims=True)
-                scale = jnp.maximum(largest, 1e-30) * (1.0079 / 32767.0)
-                scale = scale.astype(BF16).astype(F32)
-                scales.append(scale)
-                code = jnp.round(piece * (1.0 / scale)).astype(I32)
-                both = jnp.bitwise_or(
-                    jnp.left_shift(code[:, 128:], 16), jnp.bitwise_and(code[:, :128], 0xFFFF)
-                )
-                sent[h, t, parity] = both.reshape(16, 8, 128)
+            largest = jnp.maximum(
+                jnp.max(jnp.abs(real), axis=1, keepdims=True),
+                jnp.max(jnp.abs(imag), axis=1, keepdims=True),
+            )
+            scale = jnp.maximum(largest, 1e-30) * (1.0079 / 32767.0)
+            scale = scale.astype(BF16).astype(F32)
+            real, imag = coded(real, 1.0 / scale), coded(imag, 1.0 / scale)
+            imag = pltpu.roll(imag.reshape(16, 8, 128), 4, 1).reshape(128, 128)
+            sent[h, t, 0] = jnp.where(top, real, imag).reshape(16, 8, 128)
+            sent[h, t, 1] = jnp.where(top, imag, real).reshape(16, 8, 128)
             if h == 0 and t == 0:
                 pl.semaphore_wait(barrier, 38)
             if h < 2:
                 send_chunk(h, t)
-            here = lane == (row % 4) * 64 + 5 + 8 * h + 4 * ((row % 8) // 4) + t
-            scale_even = jnp.where(here, scales[0], scale_even)
-            scale_odd = jnp.where(here, scales[1], scale_odd)
+            scales = jnp.where(lane == (row % 4) * 32 + 5 + 4 * h + t, scale, scales)
         if t == 0:
             rank_col = jnp.max(
                 jnp.where(slot_row == slot_f, rank_row, 0.0), axis=1, keepdims=True
             )
-            by_slot = jnp.where(lane == (row % 4) * 64, rank_col, 0.0)
-        by_slot = jnp.where(lane == (row % 4) * 64 + 1 + t, weight_col, by_slot)
+            by_slot = jnp.where(lane == (row % 4) * 32, rank_col, 0.0)
+        by_slot = jnp.where(lane == (row % 4) * 32 + 1 + t, weight_col, by_slot)
 
     owner32, row32 = iota((32, 128), 0), iota((32, 128), 1)
-    meta = (
-        dot((row32 // 4 == owner32).astype(F32).astype(BF16), by_slot.astype(BF16))
-        + dot((2 * (row32 // 8) == owner32).astype(F32).astype(BF16), scale_even.astype(BF16))
-        + dot((2 * (row32 // 8) + 1 == owner32).astype(F32).astype(BF16), scale_odd.astype(BF16))
-    )
+    by_slot = (by_slot + scales).astype(BF16)
+    meta = dot((row32 // 4 == owner32).astype(F32).astype(BF16), by_slot)
     for o in range(32):
         meta_out[o] = meta[o : o + 1]
     for i, offset in enumerate(OFFSETS):
@@ -269,8 +266,7 @@
     held_row, held_lane = iota((256, 128), 0), iota((256, 128), 1)
     expand = (iota((256, 32), 0) // 8 == iota((256, 32), 1)).astype(F32).astype(BF16)
     info = dot(expand, meta.astype(BF16))
-    info = jnp.where(held_row % 4 < 2, info[:, :128], info[:, 128:])
-    base = (held_row % 2) * 64
+    base = (held_row % 4) * 32
     flip = bl % 2
 
     def column(k):
@@ -304,7 +300,7 @@
     for h in range(4):
         power, previous = None, None
         for t in range(times):
-            scale_col = column(5 + 8 * h + 4 * ((held_row % 8) // 4) + t)
+            scale_col = column(5 + 4 * h + t)
             pltpu.make_async_copy(
                 held.at[h, t, pl.ds(1, 31)], held.at[h, t, pl.ds(1, 31)], recv_sem.at[h, t]
             ).wait()
@@ -387,8 +383,8 @@
             pltpu.VMEM((2, rows, channels), F32),
             pltpu.VMEM((4, times, 2, 16, 8, 128), I32),
             pltpu.VMEM((4, times, 32, 8, 128), I32),
-            pltpu.VMEM((32, 1, 256), F32),
-            pltpu.VMEM((32, 1, 256), F32),
+            pltpu.VMEM((32, 1, 128), F32),
+            pltpu.VMEM((32, 1, 128), F32),
             pltpu.VMEM((2, 512, 512), BF16),
             pltpu.VMEM((4, 128, 256), F32),
             pltpu.VMEM((4, 128, 256), F32),

time: 66.9 us -> 65.3 us (0.976)
  Pallas kernels: 66.8 us -> 65.2 us
    pallas_call x1, Pallas kernels: 66 us -> 64.5 us  [per_device(): pl.pallas_call(kernel, out_shape=pltpu.VMEM((4, 8, 256), F32), in_specs=[...]
where the time goes in v3:
time: 65.3 us
  Pallas kernels  65.2 us (100%)
    pallas_call x1, Pallas kernels, per_device(): pl.pallas_call(kernel, out_shape=pltpu.VMEM((4, 8, 256), F32), in_specs=[...  64.5 us

profile of v3, /device:TPU:1, one launch (start us, length us, event | category | flops | bytes accessed | tf_op | source)
XLA Modules:
  0.0 65.3 jit_solution(15583242818792415356)
XLA Ops:
  0.0 64.5 %bandpower.1.x_ref = f32[4,8,256]{2,1,0:T(8,128)S(1)} custom-call(s32[384]{0:T(512)} %labels_hbm.1, s32[16,128]{1,0:T(8,128)} %bitcast.2, s32[4,384]{1,0:T(4,128)} %bitcast.3, f32[1,1024]{1,0:T(1,128)} %constant.8.clone.taper_hbm, f32[8,256]{1,0:T(8,128)} %constant.9.clone.twiddle_hbm, bf16[384,4,1024]{2,1,0:T(4,128)(2,1)} %vis_re.1, ...), custom_call_target="tpu_custom_call" | custom-call | tf_op jit(solution)/shard_map/bandpower/pallas_call | solution.py:371
  64.5 0.8 %interleave.1 = f32[8,1024]{1,0:T(8,128)} custom-call(f32[4,8,256]{2,1,0:T(8,128)S(1)} %bandpower.1.x_ref), custom_call_target="tpu_custom_call" | custom-call | tf_op jit(solution)/shard_map/interleave/pallas_call | solution.py:411

commit v4 on v3

--- a/solution.py
+++ b/solution.py
@@ -98,6 +98,7 @@
     z, x = bl // 4, bl % 4
     times, channels = 4, 1024
     rows = labels_ref.shape[0]
+    half = rows // 2
 
     pairs = [
         (labels_hbm, labels_ref),
@@ -106,7 +107,8 @@
         (taper_hbm, taper_ref),
         (twiddle_hbm, twiddle_ref),
         (vis_re, raw.at[0]),
-        (vis_im, raw.at[1]),
+        (vis_im.at[pl.ds(0, half)], raw.at[1, pl.ds(0, half)]),
+        (vis_im.at[pl.ds(half, half)], raw.at[1, pl.ds(half, half)]),
         (high_hbm, table.at[0]),
         (low_hbm, table.at[1]),
     ]
@@ -114,7 +116,7 @@
         pltpu.make_async_copy(source, target, load_sem.at[n])
         for n, (source, target) in enumerate(pairs)
     ]
-    for load in loads:
+    for load in loads[:8]:
         load.start()
 
     def partner(offset):
@@ -140,6 +142,8 @@
     for t in range(times):
         weight_wide = jnp.where(time_of == t, wide[1 + t : 2 + t], weight_wide)
 
+    loads[8].start()
+    loads[9].start()
     slot_f = iota((128, 1), 0).astype(F32)
     lane = iota((128, 128), 1)
     row = iota((128, 128), 0)
@@ -182,38 +186,53 @@
         out = dot(y_high, table[0]) + dot(y_low, table[0]) + dot(y_high, table[1])
         return out[:, :256], out[:, 256:]
 
-    folds = [
-        jnp.where(jnp.where(time_of == t, slot_wide, -1.0) == slot_f, weight_wide, 0.0)
-        for t in range(times)
-    ]
-
-    def fold_sums(fold):
+    folds = {}
+
+    def fold_of(t):
+        if t not in folds:
+            slot_t = jnp.where(time_of == t, slot_wide, -1.0)
+            folds[t] = jnp.where(slot_t == slot_f, weight_wide, 0.0)
+        return folds[t]
+
+    def folded(fold, part, start, count):
+        blocks = [
+            dot(
+                fold[:, 4 * start : 4 * (start + count)],
+                raw[part, start : start + count, :, 256 * j : 256 * j + 256].reshape(4 * count, 256),
+            )
+            for j in range(4)
+        ]
+        return jnp.concatenate(blocks, axis=1)
+
+    def first_sums(fold):
         fold = fold.astype(BF16)
-        both = []
-        for part in range(2):
-            if fold.shape[0] == 128:
-                loads[5 + part].wait()
-            blocks = [
-                dot(fold, raw[part, :, :, 256 * j : 256 * j + 256].reshape(4 * rows, 256))
-                for j in range(4)
-            ]
-            both.append(jnp.concatenate(blocks, axis=1) * taper_ref[...])
-        return both
+        loads[5].wait()
+        re = folded(fold, 0, 0, rows)
+        loads[6].wait()
+        im = folded(fold, 1, 0, half)
+        loads[7].wait()
+        im = im + folded(fold, 1, half, half)
+        return re * taper_ref[...], im * taper_ref[...]
+
+    def other_sums(fold):
+        fold = fold.astype(BF16)
+        return [folded(fold, part, 0, rows) * taper_ref[...] for part in range(2)]
 
     for t in range(times):
-        weight_col = jnp.sum(folds[t], axis=1, keepdims=True)
         if t == 0:
-            re, im = fold_sums(folds[0])
+            re, im = first_sums(fold_of(0))
         else:
             if t == 1:
-                sums[0], sums[1] = fold_sums(jnp.concatenate(folds[1:], axis=0))
+                sums[0], sums[1] = other_sums(
+                    jnp.concatenate([fold_of(u) for u in range(1, times)], axis=0)
+                )
             re = sums[0, 128 * t - 128 : 128 * t]
             im = sums[1, 128 * t - 128 : 128 * t]
         xr = [re[:, 256 * j : 256 * j + 256] for j in range(4)]
         xi = [im[:, 256 * j : 256 * j + 256] for j in range(4)]
         if t == 0:
-            loads[7].wait()
             loads[8].wait()
+            loads[9].wait()
         for h in range(4):
             real, imag = spectra(h, xr, xi)
             largest = jnp.maximum(
@@ -236,6 +255,7 @@
                 jnp.where(slot_row == slot_f, rank_row, 0.0), axis=1, keepdims=True
             )
             by_slot = jnp.where(lane == (row % 4) * 32, rank_col, 0.0)
+        weight_col = jnp.sum(fold_of(t), axis=1, keepdims=True)
         by_slot = jnp.where(lane == (row % 4) * 32 + 1 + t, weight_col, by_slot)
 
     owner32, row32 = iota((32, 128), 0), iota((32, 128), 1)
@@ -322,7 +342,7 @@
         edge(h).wait()
         power = power + jnp.where(tm < 7, previous * after[h], 0.0)
         parts[h] = (power[:64] + power[64:]).reshape(8, 8, 256)
-        for e in range(1, 8):
+        for e in (4, 3, 5, 2, 6, 1, 7):
             to = (tm + e) % 8
             pltpu.make_async_remote_copy(
                 src_ref=parts.at[h, to],
@@ -390,7 +410,7 @@
             pltpu.VMEM((4, 128, 256), F32),
             pltpu.VMEM((4, 8, 8, 256), F32),
             pltpu.VMEM((4, 8, 8, 256), F32),
-            dma((9,)),
+            dma((10,)),
             dma((4, times)),
             dma((4, times)),
             dma(()),

time: 65.3 us -> 65 us (level)
  no operation moved by 1% of the time
where the time goes in v4:
time: 65 us; the launch traced here: 64.9 us
  Pallas kernels  64.9 us (100%)
    pallas_call x1, Pallas kernels, per_device(): pl.pallas_call(kernel, out_shape=pltpu.VMEM((4, 8, 256), F32), in_specs=[...  64.1 us

profile of v4, /device:TPU:1, one launch (start us, length us, event | category | flops | bytes accessed | tf_op | source)
XLA Modules:
  0.0 64.9 jit_solution(14781248558074912784)
XLA Ops:
  0.0 64.1 %bandpower.1.x_ref = f32[4,8,256]{2,1,0:T(8,128)S(1)} custom-call(s32[384]{0:T(512)} %labels_hbm.1, s32[16,128]{1,0:T(8,128)} %bitcast.2, s32[4,384]{1,0:T(4,128)} %bitcast.3, f32[1,1024]{1,0:T(1,128)} %constant.8.clone.taper_hbm, f32[8,256]{1,0:T(8,128)} %constant.9.clone.twiddle_hbm, bf16[384,4,1024]{2,1,0:T(4,128)(2,1)} %vis_re.1, ...), custom_call_target="tpu_custom_call" | custom-call | tf_op jit(solution)/shard_map/bandpower/pallas_call | solution.py:391
  64.1 0.8 %interleave.1 = f32[8,1024]{1,0:T(8,128)} custom-call(f32[4,8,256]{2,1,0:T(8,128)S(1)} %bandpower.1.x_ref), custom_call_target="tpu_custom_call" | custom-call | tf_op jit(solution)/shard_map/interleave/pallas_call | solution.py:431
